TPU v7x, 512 devices: a whole 4x8x8 slice. The times are simulated.
512 devices in a mesh: row: 16 (over y, core), col: 32 (over z, x).
Axes of the slice: x: 4, y: 8, z: 8, core: 2. Of those that a mesh axis runs over, the one named last changes fastest.
Arguments:
- couplings: float32 [24576, 24576], P('row', 'col'), may hold values from -0.0390625 to 0.0390625
- diag_terms: float32 [24576], P('col'), may hold values from 1 to 4
- start_block: float32 [3, 24576], P(None, 'col'), may hold values from -6 to 6
Outputs:
- basis_scaled: float32 [2, 3, 24576], P(None, None, 'col')
- coeffs: float32 [2, 2, 3, 3], replicated
All inputs are finite; a program needn't handle non-finite values.
Results may differ from a plain program's by a relative error of at most 0.0003.
Values sent between devices are 32-bit elements; how exact they have to be, the bound alone decides.
No kernel may reach another device: no remote copies, remote signals or barrier semaphores. Data moves between devices by JAX's collectives and lax.ppermute only.
A program may use at most 64 MiB of HBM per device.

v0:
```python
import jax
import jax.numpy as jnp
from jax import lax
from jax.sharding import PartitionSpec as P

ITERS = 2
M = 24576


def turned_gather(arrays, axis, dims):
    turned = [jnp.moveaxis(a, dim, 0) for a, dim in zip(arrays, dims)]
    both = jnp.concatenate([t.reshape(len(t), -1) for t in turned], axis=1)
    result, at, done = (lax.all_gather(both, axis, axis=0, tiled=True), 0, [])
    for t, dim in zip(turned, dims):
        piece = result[:, at : at + t[0].size].reshape(-1, *t.shape[1:])
        done.append(jnp.moveaxis(piece, 0, dim))
        at += t[0].size
    return tuple(done)


def from_everyone(shard, axis):
    copies = jnp.broadcast_to(shard, (lax.axis_size(axis), *shard.shape))
    return lax.all_to_all(copies, axis, split_axis=0, concat_axis=0, tiled=True)


def over_copies(shard, axis):
    everything = from_everyone(shard, axis)
    return jnp.sum(everything, axis=0)


def in_order(tiles, dim):
    shape = list(tiles.shape[1:])
    shape[dim] *= tiles.shape[0]
    return jnp.moveaxis(tiles, 0, dim).reshape(shape)


def gathered_copies(shard, axis, dim):
    return in_order(from_everyone(shard, axis), dim)


def product(a, b):
    return jnp.dot(a, b, precision=lax.Precision.HIGHEST, preferred_element_type=jnp.float32)


def product_rows(a, matrix):
    return lax.dot_general(
        a,
        matrix,
        (((1,), (1,)), ((), ())),
        precision=lax.Precision.HIGHEST,
        preferred_element_type=jnp.float32,
    )


def shards(couplings, diag_terms, start_block):
    row_index = lax.axis_index("row")
    col_index = lax.axis_index("col")
    width_row = couplings.shape[0]
    width_col = couplings.shape[1]
    root = jnp.sqrt(jnp.float32(M))
    scaled = []
    blocks = []
    start_full, diag_full = turned_gather((start_block, diag_terms), "col", (1, 0))
    first_factor = jnp.linalg.cholesky(product(start_full, start_full.T))
    current = jax.scipy.linalg.solve_triangular(first_factor, start_full, lower=True)
    basis = [current]
    for step in range(ITERS):
        col_piece = lax.dynamic_slice_in_dim(current, col_index * width_col, width_col, 1)
        row_piece = lax.dynamic_slice_in_dim(current, row_index * width_row, width_row, 1)
        forward_rows = over_copies(product_rows(col_piece, couplings), "col")
        backward_cols = over_copies(product(row_piece, couplings), "row")
        forward = lax.all_gather(forward_rows, "row", axis=1, tiled=True)
        backward = gathered_copies(backward_cols, "col", 1)
        image = diag_full[None, :] * current + 0.5 * (forward + backward)
        prior = jnp.concatenate(basis, 0)
        correlation = product(image, prior.T)
        image = image - product(correlation, prior)
        factor = jnp.linalg.cholesky(product(image, image.T))
        current = jax.scipy.linalg.solve_triangular(factor, image, lower=True)
        basis.append(current)
        own_cols = lax.dynamic_slice_in_dim(current, col_index * width_col, width_col, 1)
        scaled.append(own_cols * root)
        blocks.append(jnp.stack([correlation[:, 3 * step : 3 * step + 3], factor]))
    return (jnp.stack(scaled), jnp.stack(blocks))


def solution(mesh):
    placed = (P("row", "col"), P("col"), P(None, "col"))
    return jax.shard_map(
        shards, mesh=mesh, in_specs=placed, out_specs=(P(None, None, "col"), P()), check_vma=False
    )
```

profile of v0, /device:TPU:1, one launch (start us, length us, event | category | flops | bytes accessed | tf_op | source)
XLA Modules:
  0.0 230.9 jit_solution(8561767828042711058)
XLA Ops:
  0.6 0.7 reshape.22
  1.3 0.7 pad_maximum_fusion.4
  2.0 44.4 %all_gather.9 = f32[24576,4]{0,1:T(4,128)S(1)} all-gather(f32[768,4]{0,1:T(4,128)S(1)} %pad_maximum_fusion.4), channel_id=1, replica_groups=mesh['row'=16,'col'=32] {'col'}, dimensions={0}, use_global_device_ids=true | all-gather | bytes 405504 | tf_op jit(solution)/shard_map/all_gather | solution.py:13
  46.5 1.8 fusion.4
  48.4 0.3 cholesky.59
  48.7 0.6 compare_reduce_fusion.2
  49.4 0.6 fusion.19
  50.0 0.3 custom-call.7
  50.3 1.0 fusion.1
  51.2 4.6 %fusion.13 = f32[3,768]{1,0:T(4,128)S(1)} fusion(f32[1536,768]{1,0:T(8,128)} %param.6, f32[3,24576]{1,0:T(4,128)S(1)} %fusion.1, s32[]{:T(128)S(6)} %select_n.14), kind=kOutput, calls=%fused_computation.19 | convolution fusion | flops 42467328 | bytes 4752388 | tf_op jit(solution)/shard_map/dot_general | solution.py:42
  55.9 0.7 broadcast_in_dim.19
  56.6 19.9 %all-to-all-start.1 = ((f32[16,3,768]{2,1,0:T(4,128)}), f32[16,3,768]{2,1,0:T(4,128)S(1)}, u32[]{:S(2)}, u32[]{:S(2)}) async-start(f32[16,3,768]{2,1,0:T(4,128)} %broadcast_in_dim.19), calls=%async_computation.1 | async-start | bytes 393216 | tf_op jit(solution)/shard_map/all_to_all | solution.py:23
  76.5 6.2 %fusion.15 = f32[3,1536]{1,0:T(4,128)S(1)} fusion(f32[1536,768]{1,0:T(8,128)} %param.6, f32[3,24576]{1,0:T(4,128)S(1)} %fusion.1, s32[]{:T(128)S(6)} %select_n.7), kind=kOutput, calls=%fused_computation.24 | convolution fusion | flops 42467328 | bytes 4749316 | tf_op jit(solution)/shard_map/dot_general | solution.py:46
  82.7 4.0 %all-to-all-done.1 = f32[16,3,768]{2,1,0:T(4,128)S(1)} async-done(((f32[16,3,768]{2,1,0:T(4,128)}), f32[16,3,768]{2,1,0:T(4,128)S(1)}, u32[]{:S(2)}, u32[]{:S(2)}) %all-to-all-start.1) | async-done | bytes 147488 | tf_op jit(solution)/shard_map/all_to_all | solution.py:23
  86.7 1.0 broadcast_in_dim.18
  87.7 4.9 %all-to-all-start = ((f32[32,3,1536]{2,1,0:T(4,128)}), f32[32,3,1536]{2,1,0:T(4,128)S(1)}, u32[]{:S(2)}, u32[]{:S(2)}) async-start(f32[32,3,1536]{2,1,0:T(4,128)} %broadcast_in_dim.18), calls=%async_computation | async-start | bytes 1572864 | tf_op jit(solution)/shard_map/all_to_all | solution.py:23
  92.7 22.3 %all-to-all-done = f32[32,3,1536]{2,1,0:T(4,128)S(1)} async-done(((f32[32,3,1536]{2,1,0:T(4,128)}), f32[32,3,1536]{2,1,0:T(4,128)S(1)}, u32[]{:S(2)}, u32[]{:S(2)}) %all-to-all-start) | async-done | bytes 589856 | tf_op jit(solution)/shard_map/all_to_all | solution.py:23
  115.0 0.8 broadcast_in_dim.20
  115.8 5.1 %all-to-all-start.2 = ((f32[32,3,768]{2,1,0:T(4,128)}), f32[32,3,768]{2,1,0:T(4,128)S(1)}, u32[]{:S(2)}, u32[]{:S(2)}) async-start(f32[32,3,768]{2,1,0:T(4,128)} %broadcast_in_dim.20), calls=%async_computation.2 | async-start | bytes 786432 | tf_op jit(solution)/shard_map/all_to_all | solution.py:23
  121.2 16.9 %all_gather.10 = f32[3,24576]{1,0:T(4,128)S(1)} all-gather(f32[3,1536]{1,0:T(4,128)S(1)} %reduce_sum.36), channel_id=1, replica_groups=mesh['row'=16,'col'=32] {'row'}, dimensions={1}, use_global_device_ids=true | all-gather | bytes 313344 | tf_op jit(solution)/shard_map/all_gather | solution.py:72
  138.1 1.8 fusion.6
  139.8 0.9 convolution_subtract_fusion
  140.8 1.8 fusion.41
  142.7 0.3 cholesky.70
  143.0 0.6 compare_reduce_fusion.1
  143.6 0.6 fusion.31
  144.3 0.3 custom-call.8
  144.6 1.0 fusion.22
  145.5 4.6 %fusion.11 = f32[3,768]{1,0:T(4,128)S(1)} fusion(f32[1536,768]{1,0:T(8,128)} %param.6, f32[3,24576]{1,0:T(4,128)S(1)} %fusion.22, s32[]{:T(128)S(6)} %select_n.14), kind=kOutput, calls=%fused_computation.17 | convolution fusion | flops 42467328 | bytes 4752388 | tf_op jit(solution)/shard_map/dot_general | solution.py:42
  150.2 0.7 broadcast_in_dim.22
  150.9 5.1 %all-to-all-start.4 = ((f32[16,3,768]{2,1,0:T(4,128)}), f32[16,3,768]{2,1,0:T(4,128)S(1)}, u32[]{:S(2)}, u32[]{:S(2)}) async-start(f32[16,3,768]{2,1,0:T(4,128)} %broadcast_in_dim.22), calls=%async_computation.4 | async-start | bytes 393216 | tf_op jit(solution)/shard_map/all_to_all | solution.py:23
  155.9 6.2 %fusion.17 = f32[3,1536]{1,0:T(4,128)S(1)} fusion(f32[1536,768]{1,0:T(8,128)} %param.6, f32[3,24576]{1,0:T(4,128)S(1)} %fusion.22, s32[]{:T(128)S(6)} %select_n.7), kind=kOutput, calls=%fused_computation.26 | convolution fusion | flops 42467328 | bytes 4749316 | tf_op jit(solution)/shard_map/dot_general | solution.py:46
  162.1 4.0 %all-to-all-done.4 = f32[16,3,768]{2,1,0:T(4,128)S(1)} async-done(((f32[16,3,768]{2,1,0:T(4,128)}), f32[16,3,768]{2,1,0:T(4,128)S(1)}, u32[]{:S(2)}, u32[]{:S(2)}) %all-to-all-start.4) | async-done | bytes 147488 | tf_op jit(solution)/shard_map/all_to_all | solution.py:23
  166.1 1.0 broadcast_in_dim.21
  167.1 9.5 %all-to-all-start.3 = ((f32[32,3,1536]{2,1,0:T(4,128)}), f32[32,3,1536]{2,1,0:T(4,128)S(1)}, u32[]{:S(2)}, u32[]{:S(2)}) async-start(f32[32,3,1536]{2,1,0:T(4,128)} %broadcast_in_dim.21), calls=%async_computation.3 | async-start | bytes 1572864 | tf_op jit(solution)/shard_map/all_to_all | solution.py:23
  176.7 22.3 %all-to-all-done.3 = f32[32,3,1536]{2,1,0:T(4,128)S(1)} async-done(((f32[32,3,1536]{2,1,0:T(4,128)}), f32[32,3,1536]{2,1,0:T(4,128)S(1)}, u32[]{:S(2)}, u32[]{:S(2)}) %all-to-all-start.3) | async-done | bytes 589856 | tf_op jit(solution)/shard_map/all_to_all | solution.py:23
  199.0 0.8 broadcast_in_dim.23
  199.8 5.1 %all-to-all-start.5 = ((f32[32,3,768]{2,1,0:T(4,128)}), f32[32,3,768]{2,1,0:T(4,128)S(1)}, u32[]{:S(2)}, u32[]{:S(2)}) async-start(f32[32,3,768]{2,1,0:T(4,128)} %broadcast_in_dim.23), calls=%async_computation.5 | async-start | bytes 786432 | tf_op jit(solution)/shard_map/all_to_all | solution.py:23
  205.1 16.9 %all_gather.11 = f32[3,24576]{1,0:T(4,128)S(1)} all-gather(f32[3,1536]{1,0:T(4,128)S(1)} %reduce_sum.38), channel_id=1, replica_groups=mesh['row'=16,'col'=32] {'row'}, dimensions={1}, use_global_device_ids=true | all-gather | bytes 313344 | tf_op jit(solution)/shard_map/all_gather | solution.py:72
  222.0 1.8 fusion
  223.8 1.0 convolution_subtract_fusion.1
  224.8 1.8 fusion.42
  226.7 0.3 cholesky.81
  227.0 0.6 compare_reduce_fusion
  227.7 0.7 fusion.32
  228.7 1.0 fusion.20
  229.7 0.6 copy.44
  230.3 0.6 pad_maximum_fusion.5
  (24 shorter events, 1.2 us)
Async XLA Ops:
  56.6 30.1 %all-to-all-start.1 = ((f32[16,3,768]{2,1,0:T(4,128)}), f32[16,3,768]{2,1,0:T(4,128)S(1)}, u32[]{:S(2)}, u32[]{:S(2)}) async-start(f32[16,3,768]{2,1,0:T(4,128)} %broadcast_in_dim.19), calls=%async_computation.1 | async-start | bytes 393216 | tf_op jit(solution)/shard_map/all_to_all | solution.py:23
  87.7 27.3 %all-to-all-start = ((f32[32,3,1536]{2,1,0:T(4,128)}), f32[32,3,1536]{2,1,0:T(4,128)S(1)}, u32[]{:S(2)}, u32[]{:S(2)}) async-start(f32[32,3,1536]{2,1,0:T(4,128)} %broadcast_in_dim.18), calls=%async_computation | async-start | bytes 1572864 | tf_op jit(solution)/shard_map/all_to_all | solution.py:23
  115.8 22.3 %all-to-all-start.2 = ((f32[32,3,768]{2,1,0:T(4,128)}), f32[32,3,768]{2,1,0:T(4,128)S(1)}, u32[]{:S(2)}, u32[]{:S(2)}) async-start(f32[32,3,768]{2,1,0:T(4,128)} %broadcast_in_dim.20), calls=%async_computation.2 | async-start | bytes 786432 | tf_op jit(solution)/shard_map/all_to_all | solution.py:23
  150.9 15.3 %all-to-all-start.4 = ((f32[16,3,768]{2,1,0:T(4,128)}), f32[16,3,768]{2,1,0:T(4,128)S(1)}, u32[]{:S(2)}, u32[]{:S(2)}) async-start(f32[16,3,768]{2,1,0:T(4,128)} %broadcast_in_dim.22), calls=%async_computation.4 | async-start | bytes 393216 | tf_op jit(solution)/shard_map/all_to_all | solution.py:23
  167.1 31.9 %all-to-all-start.3 = ((f32[32,3,1536]{2,1,0:T(4,128)}), f32[32,3,1536]{2,1,0:T(4,128)S(1)}, u32[]{:S(2)}, u32[]{:S(2)}) async-start(f32[32,3,1536]{2,1,0:T(4,128)} %broadcast_in_dim.21), calls=%async_computation.3 | async-start | bytes 1572864 | tf_op jit(solution)/shard_map/all_to_all | solution.py:23
  199.8 22.2 %all-to-all-start.5 = ((f32[32,3,768]{2,1,0:T(4,128)}), f32[32,3,768]{2,1,0:T(4,128)S(1)}, u32[]{:S(2)}, u32[]{:S(2)}) async-start(f32[32,3,768]{2,1,0:T(4,128)} %broadcast_in_dim.23), calls=%async_computation.5 | async-start | bytes 786432 | tf_op jit(solution)/shard_map/all_to_all | solution.py:23
where the time goes:
time: 232 us; the launch traced here: 231 us
  blocking collectives  78.2 us (34%)
  waiting for transfers between devices  52.7 us (23%)
  starting transfers between devices  49.7 us (21%)
  matrix products  35.4 us (15%)
  other arithmetic  7.44 us (3%)
  local copies, waits for them, and re-layouts  6.66 us (3%)
    all_to_all x6, waiting for transfers between devices, from_everyone(): return lax.all_to_all(copies, axis, split_axis=0, concat_axis=0, tiled=True)  52.7 us
    all_to_all x6, starting transfers between devices, from_everyone(): return lax.all_to_all(copies, axis, split_axis=0, concat_axis=0, tiled=True)  49.7 us
    all_gather x1, blocking collectives, turned_gather(): result, at, done = (lax.all_gather(both, axis, axis=0, tiled=True), 0, [])  44.4 us
    all_gather x2, blocking collectives, shards(): forward = lax.all_gather(forward_rows, 'row', axis=1, tiled=True)  33.8 us
    dot_general x9, matrix products, product(): jnp.dot(a, b, precision=lax.Precision.HIGHEST, preferred_element_type=jnp...  20.2 us
    dot_general x2, matrix products, product_rows(): lax.dot_general(a, matrix, (((1,), (1,)), ((), ())), precision=lax.Precis...  12.4 us
    broadcast_in_dim x6, local copies, waits for them, and re-layouts, from_everyone(): copies = jnp.broadcast_to(shard, (lax.axis_size(axis), *shard.shape))  4.95 us
  transfers between devices with their start and end apart: 6, of which 4 were waited for; matrix products, arithmetic and copies ran while one was open for 6% of the time, Pallas kernels for 0%

commit v1 on v0

--- a/solution.py
+++ b/solution.py
@@ -69,7 +69,12 @@
         row_piece = lax.dynamic_slice_in_dim(current, row_index * width_row, width_row, 1)
         forward_rows = over_copies(product_rows(col_piece, couplings), "col")
         backward_cols = over_copies(product(row_piece, couplings), "row")
-        forward = lax.all_gather(forward_rows, "row", axis=1, tiled=True)
+        forward = jnp.concatenate(
+            lax.all_to_all(
+                jnp.stack([forward_rows for _ in range(lax.axis_size("row"))], axis=0), "row", 0, 0
+            ),
+            1,
+        )
         backward = gathered_copies(backward_cols, "col", 1)
         image = diag_full[None, :] * current + 0.5 * (forward + backward)
         prior = jnp.concatenate(basis, 0)

time: 232 us -> 260 us (1.12)
  waiting for transfers between devices: 52.7 us -> 107 us
  blocking collectives: 78.2 us -> 44.4 us
  starting transfers between devices: 49.7 us -> 55.2 us
    all_gather x2 -> x0, blocking collectives: 33.8 us -> none  [shards(): forward = lax.all_gather(forward_rows, 'row', axis=1, tiled=True)]
    all_to_all x0 -> x2, waiting for transfers between devices: none -> 29.1 us  [shards(): lax.all_to_all(jnp.stack([forward_rows for _ in range(lax.axis_size('row'...]
    all_to_all x6, waiting for transfers between devices: 52.7 us -> 78.3 us  [from_everyone(): return lax.all_to_all(copies, axis, split_axis=0, concat_axis=0, tiled=True)]
    all_to_all x0 -> x2, starting transfers between devices: none -> 12.9 us  [shards(): lax.all_to_all(jnp.stack([forward_rows for _ in range(lax.axis_size('row'...]
    all_to_all x6, starting transfers between devices: 49.7 us -> 42.3 us  [from_everyone(): return lax.all_to_all(copies, axis, split_axis=0, concat_axis=0, tiled=True)]
  transfers between devices with their start and end apart: 6 -> 8, of which waited for: 4 -> 8; matrix products, arithmetic and copies ran while one was open for 6% -> 5% of each run, Pallas kernels for 0% -> 0%
where the time goes in v1:
time: 260 us; the launch traced here: 259 us
  waiting for transfers between devices  107 us (41%)
  starting transfers between devices  55.2 us (21%)
  blocking collectives  44.4 us (17%)
  matrix products  35.4 us (14%)
  local copies, waits for them, and re-layouts  8.24 us (3%)
  other arithmetic  7.44 us (3%)
    all_to_all x6, waiting for transfers between devices, from_everyone(): return lax.all_to_all(copies, axis, split_axis=0, concat_axis=0, tiled=True)  78.3 us
    all_gather x1, blocking collectives, turned_gather(): result, at, done = (lax.all_gather(both, axis, axis=0, tiled=True), 0, [])  44.4 us
    all_to_all x6, starting transfers between devices, from_everyone(): return lax.all_to_all(copies, axis, split_axis=0, concat_axis=0, tiled=True)  42.3 us
    all_to_all x2, waiting for transfers between devices, shards(): lax.all_to_all(jnp.stack([forward_rows for _ in range(lax.axis_size('row'...  29.1 us
    dot_general x9, matrix products, product(): jnp.dot(a, b, precision=lax.Precision.HIGHEST, preferred_element_type=jnp...  20.2 us
    all_to_all x2, starting transfers between devices, shards(): lax.all_to_all(jnp.stack([forward_rows for _ in range(lax.axis_size('row'...  12.9 us
    dot_general x2, matrix products, product_rows(): lax.dot_general(a, matrix, (((1,), (1,)), ((), ())), precision=lax.Precis...  12.4 us
  transfers between devices with their start and end apart: 8, of which 8 were waited for; matrix products, arithmetic and copies ran while one was open for 5% of the time, Pallas kernels for 0%

profile of v1, /device:TPU:1, one launch (start us, length us, event | category | flops | bytes accessed | tf_op | source)
XLA Modules:
  0.0 258.9 jit_solution(6205729539807314754)
XLA Ops:
  0.6 0.7 reshape.38
  1.3 0.7 pad_maximum_fusion.4
  2.0 44.4 %all_gather.3 = f32[24576,4]{0,1:T(4,128)S(1)} all-gather(f32[768,4]{0,1:T(4,128)S(1)} %pad_maximum_fusion.4), channel_id=1, replica_groups=mesh['row'=16,'col'=32] {'col'}, dimensions={0}, use_global_device_ids=true | all-gather | bytes 405504 | tf_op jit(solution)/shard_map/all_gather | solution.py:13
  46.5 1.8 fusion.4
  48.7 0.6 compare_reduce_fusion.2
  49.4 0.6 fusion.19
  50.3 1.0 fusion.1
  51.2 4.6 %fusion.13 = f32[3,768]{1,0:T(4,128)S(1)} fusion(f32[1536,768]{1,0:T(8,128)} %param.6, f32[3,24576]{1,0:T(4,128)S(1)} %fusion.1, s32[]{:T(128)S(6)} %select_n.14), kind=kOutput, calls=%fused_computation.19 | convolution fusion | flops 42467328 | bytes 4752388 | tf_op jit(solution)/shard_map/dot_general | solution.py:42
  55.9 0.7 broadcast_in_dim.19
  56.6 19.9 %all-to-all-start.2 = ((f32[16,3,768]{2,1,0:T(4,128)}), f32[16,3,768]{2,1,0:T(4,128)S(1)}, u32[]{:S(2)}, u32[]{:S(2)}) async-start(f32[16,3,768]{2,1,0:T(4,128)} %broadcast_in_dim.19), calls=%async_computation.2 | async-start | bytes 393216 | tf_op jit(solution)/shard_map/all_to_all | solution.py:23
  76.5 6.2 %fusion.15 = f32[3,1536]{1,0:T(4,128)S(1)} fusion(f32[1536,768]{1,0:T(8,128)} %param.6, f32[3,24576]{1,0:T(4,128)S(1)} %fusion.1, s32[]{:T(128)S(6)} %select_n.7), kind=kOutput, calls=%fused_computation.24 | convolution fusion | flops 42467328 | bytes 4749316 | tf_op jit(solution)/shard_map/dot_general | solution.py:46
  82.7 4.0 %all-to-all-done.2 = f32[16,3,768]{2,1,0:T(4,128)S(1)} async-done(((f32[16,3,768]{2,1,0:T(4,128)}), f32[16,3,768]{2,1,0:T(4,128)S(1)}, u32[]{:S(2)}, u32[]{:S(2)}) %all-to-all-start.2) | async-done | bytes 147488 | tf_op jit(solution)/shard_map/all_to_all | solution.py:23
  86.7 1.0 broadcast_in_dim.18
  87.7 4.9 %all-to-all-start = ((f32[32,3,1536]{2,1,0:T(4,128)}), f32[32,3,1536]{2,1,0:T(4,128)S(1)}, u32[]{:S(2)}, u32[]{:S(2)}) async-start(f32[32,3,1536]{2,1,0:T(4,128)} %broadcast_in_dim.18), calls=%async_computation | async-start | bytes 1572864 | tf_op jit(solution)/shard_map/all_to_all | solution.py:23
  92.7 22.3 %all-to-all-done = f32[32,3,1536]{2,1,0:T(4,128)S(1)} async-done(((f32[32,3,1536]{2,1,0:T(4,128)}), f32[32,3,1536]{2,1,0:T(4,128)S(1)}, u32[]{:S(2)}, u32[]{:S(2)}) %all-to-all-start) | async-done | bytes 589856 | tf_op jit(solution)/shard_map/all_to_all | solution.py:23
  115.0 0.8 broadcast_in_dim.20
  115.8 5.1 %all-to-all-start.3 = ((f32[32,3,768]{2,1,0:T(4,128)}), f32[32,3,768]{2,1,0:T(4,128)S(1)}, u32[]{:S(2)}, u32[]{:S(2)}) async-start(f32[32,3,768]{2,1,0:T(4,128)} %broadcast_in_dim.20), calls=%async_computation.3 | async-start | bytes 786432 | tf_op jit(solution)/shard_map/all_to_all | solution.py:23
  121.1 13.5 %all-to-all-done.3 = f32[32,3,768]{2,1,0:T(4,128)S(1)} async-done(((f32[32,3,768]{2,1,0:T(4,128)}), f32[32,3,768]{2,1,0:T(4,128)S(1)}, u32[]{:S(2)}, u32[]{:S(2)}) %all-to-all-start.3) | async-done | bytes 294944 | tf_op jit(solution)/shard_map/all_to_all | solution.py:23
  134.5 0.8 stack.28
  135.3 6.1 %all-to-all-start.1 = ((f32[16,3,1536]{2,1,0:T(4,128)}), f32[16,3,1536]{2,1,0:T(4,128)S(1)}, u32[]{:S(2)}, u32[]{:S(2)}) async-start(f32[16,3,1536]{2,1,0:T(4,128)} %stack.28), calls=%async_computation.1 | async-start | bytes 786432 | tf_op jit(solution)/shard_map/all_to_all | solution.py:73
  141.6 14.5 %all-to-all-done.1 = f32[16,3,1536]{2,1,0:T(4,128)S(1)} async-done(((f32[16,3,1536]{2,1,0:T(4,128)}), f32[16,3,1536]{2,1,0:T(4,128)S(1)}, u32[]{:S(2)}, u32[]{:S(2)}) %all-to-all-start.1) | async-done | bytes 294944 | tf_op jit(solution)/shard_map/all_to_all | solution.py:73
  156.1 1.8 fusion.6
  157.9 0.9 convolution_subtract_fusion
  158.8 1.8 fusion.41
  161.0 0.6 compare_reduce_fusion.1
  161.7 0.6 fusion.31
  162.6 1.0 fusion.22
  163.6 4.6 %fusion.11 = f32[3,768]{1,0:T(4,128)S(1)} fusion(f32[1536,768]{1,0:T(8,128)} %param.6, f32[3,24576]{1,0:T(4,128)S(1)} %fusion.22, s32[]{:T(128)S(6)} %select_n.14), kind=kOutput, calls=%fused_computation.17 | convolution fusion | flops 42467328 | bytes 4752388 | tf_op jit(solution)/shard_map/dot_general | solution.py:42
  168.2 0.7 broadcast_in_dim.22
  168.9 3.4 %all-to-all-start.6 = ((f32[16,3,768]{2,1,0:T(4,128)}), f32[16,3,768]{2,1,0:T(4,128)S(1)}, u32[]{:S(2)}, u32[]{:S(2)}) async-start(f32[16,3,768]{2,1,0:T(4,128)} %broadcast_in_dim.22), calls=%async_computation.6 | async-start | bytes 393216 | tf_op jit(solution)/shard_map/all_to_all | solution.py:23
  172.3 6.2 %fusion.17 = f32[3,1536]{1,0:T(4,128)S(1)} fusion(f32[1536,768]{1,0:T(8,128)} %param.6, f32[3,24576]{1,0:T(4,128)S(1)} %fusion.22, s32[]{:T(128)S(6)} %select_n.7), kind=kOutput, calls=%fused_computation.26 | convolution fusion | flops 42467328 | bytes 4749316 | tf_op jit(solution)/shard_map/dot_general | solution.py:46
  178.5 3.4 %all-to-all-done.6 = f32[16,3,768]{2,1,0:T(4,128)S(1)} async-done(((f32[16,3,768]{2,1,0:T(4,128)}), f32[16,3,768]{2,1,0:T(4,128)S(1)}, u32[]{:S(2)}, u32[]{:S(2)}) %all-to-all-start.6) | async-done | bytes 147488 | tf_op jit(solution)/shard_map/all_to_all | solution.py:23
  181.9 1.0 broadcast_in_dim.21
  182.9 3.9 %all-to-all-start.4 = ((f32[32,3,1536]{2,1,0:T(4,128)}), f32[32,3,1536]{2,1,0:T(4,128)S(1)}, u32[]{:S(2)}, u32[]{:S(2)}) async-start(f32[32,3,1536]{2,1,0:T(4,128)} %broadcast_in_dim.21), calls=%async_computation.4 | async-start | bytes 1572864 | tf_op jit(solution)/shard_map/all_to_all | solution.py:23
  186.9 22.3 %all-to-all-done.4 = f32[32,3,1536]{2,1,0:T(4,128)S(1)} async-done(((f32[32,3,1536]{2,1,0:T(4,128)}), f32[32,3,1536]{2,1,0:T(4,128)S(1)}, u32[]{:S(2)}, u32[]{:S(2)}) %all-to-all-start.4) | async-done | bytes 589856 | tf_op jit(solution)/shard_map/all_to_all | solution.py:23
  209.1 0.8 broadcast_in_dim.23
  209.9 5.0 %all-to-all-start.7 = ((f32[32,3,768]{2,1,0:T(4,128)}), f32[32,3,768]{2,1,0:T(4,128)S(1)}, u32[]{:S(2)}, u32[]{:S(2)}) async-start(f32[32,3,768]{2,1,0:T(4,128)} %broadcast_in_dim.23), calls=%async_computation.7 | async-start | bytes 786432 | tf_op jit(solution)/shard_map/all_to_all | solution.py:23
  215.1 12.8 %all-to-all-done.7 = f32[32,3,768]{2,1,0:T(4,128)S(1)} async-done(((f32[32,3,768]{2,1,0:T(4,128)}), f32[32,3,768]{2,1,0:T(4,128)S(1)}, u32[]{:S(2)}, u32[]{:S(2)}) %all-to-all-start.7) | async-done | bytes 294944 | tf_op jit(solution)/shard_map/all_to_all | solution.py:23
  227.9 0.8 stack.30
  228.7 6.7 %all-to-all-start.5 = ((f32[16,3,1536]{2,1,0:T(4,128)}), f32[16,3,1536]{2,1,0:T(4,128)S(1)}, u32[]{:S(2)}, u32[]{:S(2)}) async-start(f32[16,3,1536]{2,1,0:T(4,128)} %stack.30), calls=%async_computation.5 | async-start | bytes 786432 | tf_op jit(solution)/shard_map/all_to_all | solution.py:73
  235.5 14.6 %all-to-all-done.5 = f32[16,3,1536]{2,1,0:T(4,128)S(1)} async-done(((f32[16,3,1536]{2,1,0:T(4,128)}), f32[16,3,1536]{2,1,0:T(4,128)S(1)}, u32[]{:S(2)}, u32[]{:S(2)}) %all-to-all-start.5) | async-done | bytes 294944 | tf_op jit(solution)/shard_map/all_to_all | solution.py:73
  250.0 1.8 fusion
  251.8 1.0 convolution_subtract_fusion.1
  252.8 1.8 fusion.42
  255.0 0.6 compare_reduce_fusion
  255.7 0.7 fusion.32
  256.7 1.0 fusion.20
  257.7 0.6 copy.44
  (28 shorter events, 3.2 us)
Async XLA Ops:
  56.6 30.1 %all-to-all-start.2 = ((f32[16,3,768]{2,1,0:T(4,128)}), f32[16,3,768]{2,1,0:T(4,128)S(1)}, u32[]{:S(2)}, u32[]{:S(2)}) async-start(f32[16,3,768]{2,1,0:T(4,128)} %broadcast_in_dim.19), calls=%async_computation.2 | async-start | bytes 393216 | tf_op jit(solution)/shard_map/all_to_all | solution.py:23
  87.7 27.3 %all-to-all-start = ((f32[32,3,1536]{2,1,0:T(4,128)}), f32[32,3,1536]{2,1,0:T(4,128)S(1)}, u32[]{:S(2)}, u32[]{:S(2)}) async-start(f32[32,3,1536]{2,1,0:T(4,128)} %broadcast_in_dim.18), calls=%async_computation | async-start | bytes 1572864 | tf_op jit(solution)/shard_map/all_to_all | solution.py:23
  115.8 18.8 %all-to-all-start.3 = ((f32[32,3,768]{2,1,0:T(4,128)}), f32[32,3,768]{2,1,0:T(4,128)S(1)}, u32[]{:S(2)}, u32[]{:S(2)}) async-start(f32[32,3,768]{2,1,0:T(4,128)} %broadcast_in_dim.20), calls=%async_computation.3 | async-start | bytes 786432 | tf_op jit(solution)/shard_map/all_to_all | solution.py:23
  135.3 20.8 %all-to-all-start.1 = ((f32[16,3,1536]{2,1,0:T(4,128)}), f32[16,3,1536]{2,1,0:T(4,128)S(1)}, u32[]{:S(2)}, u32[]{:S(2)}) async-start(f32[16,3,1536]{2,1,0:T(4,128)} %stack.28), calls=%async_computation.1 | async-start | bytes 786432 | tf_op jit(solution)/shard_map/all_to_all | solution.py:73
  168.9 13.0 %all-to-all-start.6 = ((f32[16,3,768]{2,1,0:T(4,128)}), f32[16,3,768]{2,1,0:T(4,128)S(1)}, u32[]{:S(2)}, u32[]{:S(2)}) async-start(f32[16,3,768]{2,1,0:T(4,128)} %broadcast_in_dim.22), calls=%async_computation.6 | async-start | bytes 393216 | tf_op jit(solution)/shard_map/all_to_all | solution.py:23
  182.9 26.2 %all-to-all-start.4 = ((f32[32,3,1536]{2,1,0:T(4,128)}), f32[32,3,1536]{2,1,0:T(4,128)S(1)}, u32[]{:S(2)}, u32[]{:S(2)}) async-start(f32[32,3,1536]{2,1,0:T(4,128)} %broadcast_in_dim.21), calls=%async_computation.4 | async-start | bytes 1572864 | tf_op jit(solution)/shard_map/all_to_all | solution.py:23
  209.9 18.0 %all-to-all-start.7 = ((f32[32,3,768]{2,1,0:T(4,128)}), f32[32,3,768]{2,1,0:T(4,128)S(1)}, u32[]{:S(2)}, u32[]{:S(2)}) async-start(f32[32,3,768]{2,1,0:T(4,128)} %broadcast_in_dim.23), calls=%async_computation.7 | async-start | bytes 786432 | tf_op jit(solution)/shard_map/all_to_all | solution.py:23
  228.7 21.3 %all-to-all-start.5 = ((f32[16,3,1536]{2,1,0:T(4,128)}), f32[16,3,1536]{2,1,0:T(4,128)S(1)}, u32[]{:S(2)}, u32[]{:S(2)}) async-start(f32[16,3,1536]{2,1,0:T(4,128)} %stack.30), calls=%async_computation.5 | async-start | bytes 786432 | tf_op jit(solution)/shard_map/all_to_all | solution.py:73
